TPU v7x, 128 devices: a whole 4x4x4 slice. The times are simulated.
128 devices in a mesh: row: 16 (over z, y), col: 8 (over x, core).
Axes of the slice: x: 4, y: 4, z: 4, core: 2. Of those that a mesh axis runs over, the one named last changes fastest.
Arguments:
- grads: float32 [64, 20, 3, 16384], P(None, None, None, ('row', 'col')), may hold values from -6 to 6
- weights: float32 [64, 16384], P(None, ('row', 'col')), may hold values from 0.005 to 0.05
- counts: int32 [16384], P(('row', 'col')), may hold values from 1 to 8
- lame_first: float32 [16384], P(('row', 'col')), may hold values from 0.5 to 2
- shear: float32 [16384], P(('row', 'col')), may hold values from 0.5 to 2
- dest_owner: int32 [16384, 1], P(('row', 'col')), may hold values from 0 to 127; in each aligned block of 128 rows (0 to 127, 128 to 255, ...) at most 2 rows name the same one
- dest_slot: int32 [16384], P(('row', 'col')), may hold values from 0 to 127
Outputs:
- assembled: float32 [60, 60, 16384], P(None, None, ('row', 'col'))
Inputs may be any that keep to these rules, and one draw needn't show every extreme that they name: `dest_owner`: among the elements of one device, at most 2 have the same owner; in some device exactly 2 do.
All inputs are finite; a program needn't handle non-finite values.
Results may differ from a plain program's by a relative error of at most 0.0001.
Values sent between devices are 32-bit elements; how exact they have to be, the bound alone decides.
A program may use at most 64 MiB of HBM per device.

v0:
```python
import functools

import jax
import jax.numpy as jnp
import numpy as np
from jax import lax
from jax.sharding import Mesh
from jax.sharding import PartitionSpec as P

NF = 20
NDOF = 60
GP = 8
Q = 64
SLOTS_DEV = 128
ROW_COL = ("row_0", "row_1", "col_0", "col_1")
ROW = ("row_0", "row_1")
COL = ("col_0", "col_1")


def one_axis_at_a_time(value, axes):
    return functools.reduce(lax.psum, axes, value)


def stiffness(gflat, weff, lame_first, shear):
    count = gflat.shape[2]
    moment = jnp.einsum(
        "qme,qne->mne", gflat * weff[:, None, :], gflat, precision=lax.Precision.HIGHEST
    )
    blocks = moment.reshape(NF, 3, NF, 3, count)
    across = jnp.einsum("akbke->abe", blocks)
    eye = jnp.eye(3, dtype=jnp.float32)
    result = lame_first * blocks + shear * (
        eye[None, :, None, :, None] * across[:, None, :, None, :]
        + jnp.transpose(blocks, (0, 3, 2, 1, 4))
    )
    return result.reshape(NDOF * NDOF, count)


def triangle_tables(order):
    upper_rows, upper_cols = np.triu_indices(order)
    lookup = np.zeros((order, order), np.int32)
    lookup[upper_rows, upper_cols] = np.arange(upper_rows.shape[0], dtype=np.int32)
    lookup[upper_cols, upper_rows] = np.arange(upper_rows.shape[0], dtype=np.int32)
    upper_index = (upper_rows * order + upper_cols).astype(np.int32)
    return (upper_index, lookup.reshape(order * order))


def deliver(payload, slotcol):
    return (
        lax.all_to_all(payload, ROW_COL, split_axis=1, concat_axis=1, tiled=True),
        lax.all_to_all(slotcol, ROW_COL, split_axis=1, concat_axis=1, tiled=True),
    )


def shards(grads, weights, counts, lame_first, shear, dest_owner, dest_slot):
    count = grads.shape[3]
    nrow = lax.axis_size(ROW)
    ncol = lax.axis_size(COL)
    ndevices = nrow * ncol
    capacity = max(2, 2 * count // ndevices)
    width = ndevices * capacity
    points = lax.broadcasted_iota(jnp.int32, weights.shape, 0)
    weff = jnp.where(points < counts[None, :] * GP, weights, jnp.float32(0.0))
    squares = jnp.sum(grads * grads, axis=(1, 2))
    local_trace = jnp.sum((lame_first + 4.0 * shear) * jnp.sum(weff * squares, axis=0))
    total = one_axis_at_a_time(local_trace, ROW_COL)
    scale = total / (NDOF * count * ndevices)
    owner = dest_owner[:, 0]
    onehot = (owner[:, None] == lax.broadcasted_iota(jnp.int32, (count, ndevices), 1)).astype(
        jnp.int32
    )
    ranking = jnp.sum(jnp.cumsum(onehot, axis=0) * onehot, axis=1) - 1
    position = owner * capacity + ranking
    slotcol = (
        jnp.full((1, width), -1.0, jnp.float32).at[0, position].set(dest_slot.astype(jnp.float32))
    )
    gflat = grads.reshape(Q, NDOF, count)
    upper_index, mirror_index = triangle_tables(NDOF)
    local_blocks = stiffness(gflat, weff, lame_first, shear)
    upper_part = jnp.take(local_blocks, jnp.asarray(upper_index, jnp.int32), axis=0)
    payload = jnp.zeros((upper_part.shape[0], width), jnp.float32).at[:, position].set(upper_part)
    moved, slots_in = deliver(payload, slotcol)
    received = jnp.take(moved, jnp.asarray(mirror_index, jnp.int32), axis=0)
    slot_ids = slots_in[0].astype(jnp.int32)
    placing = (slot_ids[:, None] == lax.broadcasted_iota(jnp.int32, (width, SLOTS_DEV), 1)).astype(
        jnp.float32
    )
    summed = jnp.dot(
        received, placing, precision=lax.Precision.HIGHEST, preferred_element_type=jnp.float32
    )
    return (summed / scale).reshape(NDOF, NDOF, SLOTS_DEV)


def solution(mesh):
    split = Mesh(mesh.devices.reshape(4, 4, 4, 2), ("row_0", "row_1", "col_0", "col_1"))
    return jax.shard_map(
        shards,
        mesh=split,
        in_specs=(
            P(None, None, None, ROW_COL),
            P(None, ROW_COL),
            P(ROW_COL),
            P(ROW_COL),
            P(ROW_COL),
            P(ROW_COL, None),
            P(ROW_COL),
        ),
        out_specs=P(None, None, ROW_COL),
        check_vma=False,
    )
```

profile of v0, /device:TPU:1, one launch (start us, length us, event | category | flops | bytes accessed | tf_op | source)
XLA Modules:
  0.0 139.7 jit_solution(15029597401895756653)
XLA Ops:
  0.0 0.9 fusion.11
  1.1 0.8 select_reduce_fusion.1
  1.9 0.7 fusion.14
  2.6 0.7 convert_element_type.26
  3.2 1.0 scatter_custom_fusion.1
  4.2 0.8 all_to_all.17
  5.0 11.5 %all-to-all-start.1 = ((f32[1,128,2]{2,0,1:T(1,128)}), f32[1,128,2]{2,0,1:T(1,128)S(1)}, u32[]{:S(2)}, u32[]{:S(2)}) async-start(f32[1,128,2]{2,0,1:T(1,128)} %bitcast.7), calls=%async_computation.1 | async-start | bytes 131072 | tf_op jit(solution)/shard_map/all_to_all | solution.py:51
  16.5 1.7 %multiply_reduce_fusion = f32[64,128]{1,0:T(8,128)S(1)} fusion(f32[64,20,3,128]{3,0,2,1:T(8,128)} %param.9), kind=kLoop, calls=%fused_computation.14 | loop fusion | flops 974848 | bytes 1998848 | tf_op jit(solution)/shard_map/reduce_sum | solution.py:64
  18.4 4.7 %copy.35 = f32[64,60,128]{0,1,2:T(8,128)} copy(f32[64,60,128]{2,0,1:T(8,128)S(1)} %bitcast.24) | data formatting | bytes 3932160 | tf_op jit(solution)/shard_map/reshape | solution.py:77
  23.1 12.3 %fusion.4 = f32[60,60,128]{1,0,2:T(8,128)} fusion(f32[64,60,128]{0,1,2:T(8,128)} %copy.35, f32[64,128]{0,1:T(8,128)S(1)} %copy.34), kind=kOutput, calls=%fused_computation.12 | convolution fusion | flops 354385920 | bytes 3842048 | tf_op jit(solution)/shard_map/qme,qne->mne/dot_general | solution.py:26
  35.4 4.7 %copy.37 = f32[60,60,128]{2,1,0:T(8,128)} copy(f32[60,60,128]{1,0,2:T(8,128)} %fusion.4) | data formatting | bytes 3686400 | tf_op jit(solution)/shard_map/qme,qne->mne/transpose | solution.py:26
  40.1 3.0 %reshape.57 = f32[20,3,20,3,128]{4,3,2,1,0:T(4,128)S(1)} reshape(f32[60,60,128]{2,1,0:T(8,128)} %copy.37) | data formatting | bytes 3686400 | tf_op jit(solution)/shard_map/reshape | solution.py:29
  43.1 0.9 select_reduce_fusion
  44.1 0.5 fusion.3
  44.5 0.2 copy-done.3
  44.8 2.1 %copy.40 = f32[20,3,20,3,128]{4,3,2,1,0:T(4,128)} copy(f32[20,3,20,3,128]{4,2,3,1,0:T(8,128)S(1)} %fusion.3) | data formatting | bytes 3686400 | tf_op jit(solution)/shard_map/add | solution.py:32
  46.8 2.9 %reshape.58 = f32[3600,128]{1,0:T(8,128)S(1)} reshape(f32[20,3,20,3,128]{4,3,2,1,0:T(4,128)} %copy.40) | data formatting | bytes 3686400 | tf_op jit(solution)/shard_map/reshape | solution.py:36
  49.8 3.4 %gather_fusion = f32[1830,128]{1,0:T(8,128)S(1)} fusion(f32[3600,128]{1,0:T(8,128)S(1)} %reshape.58, s32[2048]{0:T(1024)S(1)} %pad_clamp_fusion.1), kind=kCustom, calls=%fused_computation | custom fusion | bytes 1881240 | tf_op jit(solution)/shard_map/jit(_take)/gather | solution.py:80
  53.2 1.3 copy.41
  54.5 2.3 %scatter_custom_fusion = f32[1830,256]{0,1:T(8,128)S(1)} fusion(s32[128]{0:T(128)S(1)} %fusion.14, f32[128,1830]{1,0:T(8,128)} %copy.41, f32[]{:T(128)} %constant.29.clone.1), kind=kCustom, calls=%fused_computation.15 | custom fusion | bytes 1874432 | tf_op jit(solution)/shard_map/scatter | solution.py:81
  56.8 2.4 %all_to_all.14 = f32[1830,128,2]{0,2,1:T(2,128)} reshape(f32[1830,256]{0,1:T(8,128)S(1)} %scatter_custom_fusion) | data formatting | bytes 3747840 | tf_op jit(solution)/shard_map/all_to_all | solution.py:50
  59.3 9.8 %all-to-all-start = ((f32[1830,128,2]{0,2,1:T(2,128)}), f32[1830,128,2]{0,2,1:T(2,128)S(1)}, u32[]{:S(2)}, u32[]{:S(2)}) async-start(f32[1830,128,2]{0,2,1:T(2,128)} %all_to_all.14), calls=%async_computation | async-start | bytes 3932160 | tf_op jit(solution)/shard_map/all_to_all | solution.py:50
  69.0 0.7 multiply_reduce_fusion.2
  69.7 12.2 %psum.28 = f32[]{:T(128)} all-reduce(f32[]{:T(128)} %multiply_reduce_fusion.2), channel_id=1, replica_groups=mesh['row_0'=4,'row_1'=4,'col_0'=4,'col_1'=2] {'row_0'}, use_global_device_ids=true, to_apply=%region_8.9 | all-reduce | flops 1 | bytes 8 | tf_op jit(solution)/shard_map/psum | solution.py:21
  81.9 14.9 %psum.29 = f32[]{:T(128)} all-reduce(f32[]{:T(128)} %psum.28), channel_id=1, replica_groups=mesh['row_0'=4,'row_1'=4,'col_0'=4,'col_1'=2] {'row_1'}, use_global_device_ids=true, to_apply=%region_9.10 | all-reduce | flops 1 | bytes 8 | tf_op jit(solution)/shard_map/psum | solution.py:21
  96.8 14.8 %psum.30 = f32[]{:T(128)} all-reduce(f32[]{:T(128)} %psum.29), channel_id=1, replica_groups=mesh['row_0'=4,'row_1'=4,'col_0'=4,'col_1'=2] {'col_0'}, use_global_device_ids=true, to_apply=%region_10.11 | all-reduce | flops 1 | bytes 8 | tf_op jit(solution)/shard_map/psum | solution.py:21
  111.6 7.3 %psum.31 = f32[]{:T(128)} all-reduce(f32[]{:T(128)} %psum.30), channel_id=1, replica_groups=mesh['row_0'=4,'row_1'=4,'col_0'=4,'col_1'=2] {'col_1'}, use_global_device_ids=true, to_apply=%region_11.12 | all-reduce | flops 1 | bytes 8 | tf_op jit(solution)/shard_map/psum | solution.py:21
  120.0 2.6 %all_to_all.16 = f32[1830,256]{0,1:T(8,128)} reshape(f32[1830,128,2]{0,2,1:T(2,128)S(1)} %all-to-all-done) | data formatting | bytes 3747840 | tf_op jit(solution)/shard_map/all_to_all | solution.py:50
  122.6 1.8 %copy.42 = f32[1830,256]{1,0:T(8,128)S(1)} copy(f32[1830,256]{0,1:T(8,128)} %all_to_all.16) | data formatting | bytes 3747840 | tf_op jit(solution)/shard_map/all_to_all | solution.py:50
  124.5 10.0 %gather_fusion.1 = f32[3600,256]{1,0:T(8,128)} fusion(f32[1830,256]{1,0:T(8,128)S(1)} %copy.42, s32[4096]{0:T(1024)S(1)} %pad_clamp_fusion), kind=kCustom, calls=%fused_computation.1 | custom fusion | bytes 7387200 | tf_op jit(solution)/shard_map/jit(_take)/gather | solution.py:83
  134.5 3.9 %convolution_divide_fusion = f32[3600,128]{1,0:T(8,128)S(1)} fusion(f32[3600,256]{1,0:T(8,128)} %gather_fusion.1, f32[]{:T(128)S(6)} %div.9, s32[256]{0:T(256)S(1)} %convert_element_type.28), kind=kOutput, calls=%fused_computation.6 | convolution fusion | flops 1416071168 | bytes 5530628 | tf_op jit(solution)/shard_map/dot_general | solution.py:88
  138.3 1.4 %reshape.59 = f32[60,60,128]{2,1,0:T(8,128)} reshape(f32[3600,128]{1,0:T(8,128)S(1)} %convolution_divide_fusion) | data formatting | bytes 3686400 | tf_op jit(solution)/shard_map/reshape | solution.py:91
  (25 shorter events, 0.7 us)
Async XLA Ops:
  0.0 18.4 %copy-start = (f32[64,20,3,128]{3,0,2,1:T(8,128)S(1)}, f32[64,20,3,128]{3,0,2,1:T(8,128)}, u32[]{:S(2)}) copy-start(f32[64,20,3,128]{3,0,2,1:T(8,128)} %param.9) | copy-start | bytes 5898244
  0.0 18.2 %copy-start.6 = (s32[128]{0:T(128)S(1)}, s32[128]{0:T(128)}, u32[]{:S(2)}) copy-start(s32[128]{0:T(128)} %param.11) | copy-start | bytes 1540
  0.0 18.2 %copy-start.1 = (f32[64,128]{1,0:T(8,128)S(1)}, f32[64,128]{1,0:T(8,128)}, u32[]{:S(2)}) copy-start(f32[64,128]{1,0:T(8,128)} %param.10) | copy-start | bytes 98308
  5.0 54.3 %all-to-all-start.1 = ((f32[1,128,2]{2,0,1:T(1,128)}), f32[1,128,2]{2,0,1:T(1,128)S(1)}, u32[]{:S(2)}, u32[]{:S(2)}) async-start(f32[1,128,2]{2,0,1:T(1,128)} %bitcast.7), calls=%async_computation.1 | async-start | bytes 131072 | tf_op jit(solution)/shard_map/all_to_all | solution.py:51
  43.1 0.9 copy-start.4
  43.1 0.9 copy-start.5
  44.0 0.7 copy-start.3
  59.2 60.4 %copy-start.2 = (s32[3600]{0:T(1024)S(1)}, s32[3600]{0:T(1024)}, u32[]{:S(2)}) copy-start(s32[3600]{0:T(1024)} %constant.84) | copy-start | bytes 43204
  59.3 60.7 %all-to-all-start = ((f32[1830,128,2]{0,2,1:T(2,128)}), f32[1830,128,2]{0,2,1:T(2,128)S(1)}, u32[]{:S(2)}, u32[]{:S(2)}) async-start(f32[1830,128,2]{0,2,1:T(2,128)} %all_to_all.14), calls=%async_computation | async-start | bytes 3932160 | tf_op jit(solution)/shard_map/all_to_all | solution.py:50
where the time goes:
time: 140 us
  blocking collectives  49.2 us (35%)
  local copies, waits for them, and re-layouts  44.9 us (32%)
  starting transfers between devices  21.2 us (15%)
  matrix products  16.2 us (12%)
  other arithmetic  7.21 us (5%)
    psum x4, blocking collectives, one_axis_at_a_time(): return functools.reduce(lax.psum, axes, value)  49.2 us
    dot_general x1, matrix products, stiffness(): jnp.einsum('qme,qne->mne', gflat * weff[:, None, :], gflat, precision=lax...  12.3 us
    all_to_all x1, starting transfers between devices, deliver(): lax.all_to_all(slotcol, ROW_COL, split_axis=1, concat_axis=1, tiled=True)  11.5 us
    gather x1, local copies, waits for them, and re-layouts, shards(): received = jnp.take(moved, jnp.asarray(mirror_index, jnp.int32), axis=0)  9.98 us
    all_to_all x1, starting transfers between devices, deliver(): lax.all_to_all(payload, ROW_COL, split_axis=1, concat_axis=1, tiled=True)  9.76 us
    all_to_all x3, local copies, waits for them, and re-layouts, deliver(): lax.all_to_all(payload, ROW_COL, split_axis=1, concat_axis=1, tiled=True)  6.9 us
    transpose x1, local copies, waits for them, and re-layouts, stiffness(): jnp.einsum('qme,qne->mne', gflat * weff[:, None, :], gflat, precision=lax...  4.73 us
    gather x2, local copies, waits for them, and re-layouts, shards(): jnp.take(local_blocks, jnp.asarray(upper_index, jnp.int32), axis=0)  4.7 us
  transfers between devices with their start and end apart: 2, of which 0 were waited for; matrix products, arithmetic and copies ran while one was open for 29% of the time, Pallas kernels for 0%

commit v1 on v0

v1 whole, which is shorter than its diff:
```python
import functools

import jax
import jax.numpy as jnp
from jax import lax
from jax.experimental import pallas as pl
from jax.experimental.pallas import tpu as pltpu
from jax.sharding import PartitionSpec as P

NF = 20
NDOF = 60
Q = 64
NQB = 8
LANES = 128
CAP = 2
CHUNK = 512
ROWS = (8, 8, 8, 6)
PITCH = 20
OPITCH = 72
MESH = pl.DeviceIdType.MESH


def segments():
    table, row = {}, 1
    for a in range(NF):
        for i in range(3):
            for j in range(3):
                skip = 1 if i > j else 0
                table[a, i, j] = (row, skip)
                row += NF - a - skip
    return table, row


SEGMENTS, NWORDS = segments()
WORDS = 64 * CAP * 15
TRACE_LANE = NWORDS % LANES


def split_high_low(x, axis):
    high = x.astype(jnp.bfloat16)
    low = (x - high.astype(jnp.float32)).astype(jnp.bfloat16)
    return jnp.concatenate([high, low], axis=axis)


def exchange_kernel(
    ndev, ncol,
    grads_ref, weights_ref, counts_ref, lame_ref, shear_ref, owner_ref, slot_ref,
    placed_ref, total_ref,
    gbuf, gsem, weff, partial, kmat, permute, place, sendbuf, recvbuf, send_sem, recv_sem,
):
    row, col = lax.axis_index("row"), lax.axis_index("col")
    me = row * ncol + col

    barrier = pltpu.get_barrier_semaphore()

    def greet(k, carry):
        peer = lax.rem(me + k, ndev)
        pl.semaphore_signal(
            barrier, inc=1, device_id=(peer // ncol, lax.rem(peer, ncol)), device_id_type=MESH
        )
        return carry

    lax.fori_loop(1, ndev, greet, 0)

    load = pltpu.make_async_copy(grads_ref, gbuf, gsem)
    load.start()

    owner = owner_ref[...].astype(jnp.float32)
    wide = jnp.broadcast_to(owner, (LANES, LANES))
    rows_iota = lax.broadcasted_iota(jnp.int32, (LANES, LANES), 0)
    lane_iota = lax.broadcasted_iota(jnp.int32, (LANES, LANES), 1)
    same = jnp.where((wide.T == wide) & (rows_iota < lane_iota), 1.0, 0.0)
    rank = jnp.sum(same, axis=0, keepdims=True)
    here = rows_iota.astype(jnp.float32) == wide
    for r in range(CAP):
        onehot = jnp.where(here & (rank == float(r)), 1.0, 0.0).astype(jnp.bfloat16)
        permute[pl.ds(r * LANES, LANES), pl.ds(0, LANES)] = onehot
        permute[pl.ds(r * LANES, LANES), pl.ds(LANES, LANES)] = onehot

    counts = counts_ref[...]
    for qb in range(NQB):
        weff[pl.ds(8 * qb, 8), :] = jnp.where(
            counts > qb, weights_ref[pl.ds(8 * qb, 8), :], 0.0
        )
    lame, shear = lame_ref[...], shear_ref[...]
    kmat[pl.ds(0, 1), :] = slot_ref[...].astype(jnp.float32) + 1.0
    kmat[pl.ds(NWORDS, WORDS - NWORDS), :] = jnp.zeros((WORDS - NWORDS, LANES), jnp.float32)

    load.wait()

    def moments(a):
        gw = [
            [gbuf[3 * a + i, pl.ds(8 * qb, 8), :] * weff[pl.ds(8 * qb, 8), :] for qb in range(NQB)]
            for i in range(3)
        ]

        def one(b, carry):
            acc = [[None] * 3 for _ in range(3)]
            for qb in range(NQB):
                g = [gbuf[3 * b + j, pl.ds(8 * qb, 8), :] for j in range(3)]
                for i in range(3):
                    for j in range(3):
                        term = gw[i][qb] * g[j]
                        acc[i][j] = term if qb == 0 else acc[i][j] + term
            for i in range(3):
                for j in range(3):
                    partial[pl.ds((3 * i + j) * 8 * PITCH + b, 8, stride=PITCH), :] = acc[i][j]
            return carry

        lax.fori_loop(a, NF, one, 0)
        n = NF - a
        m = [[None] * 3 for _ in range(3)]
        for i in range(3):
            for j in range(3):
                base = (3 * i + j) * 8 * PITCH + a
                total = partial[pl.ds(base, n), :]
                for s in range(1, 8):
                    total = total + partial[pl.ds(base + s * PITCH, n), :]
                m[i][j] = total
        across = m[0][0] + m[1][1] + m[2][2]
        for i in range(3):
            for j in range(3):
                start, skip = SEGMENTS[a, i, j]
                if n == skip:
                    continue
                k = lame * m[i][j] + shear * (m[j][i] + across if i == j else m[j][i])
                kmat[pl.ds(start, n - skip), :] = k[skip:]
        return across[0:1]

    def pack(c, local_total):
        for j in range(ROWS[c] // CAP):
            words = kmat[pl.ds(c * CHUNK + j * LANES, LANES), :]
            out = lax.dot_general(
                permute[...], split_high_low(words, 1), (((1,), (1,)), ((), ())),
                preferred_element_type=jnp.float32,
            )
            for r in range(CAP):
                part = out[r * LANES:(r + 1) * LANES]
                if r == 0 and c == NWORDS // CHUNK and j == NWORDS % CHUNK // LANES:
                    part = jnp.where(lane_iota == TRACE_LANE, local_total, part)
                sendbuf[c, pl.ds(CAP * j + r, LANES, stride=8), :] = part
        own = pl.multiple_of(me * 8, 8)
        recvbuf[c, pl.ds(own, 8), :] = sendbuf[c, pl.ds(own, 8), :]

    def send(c):
        def one(k, carry):
            peer = lax.rem(me + lax.rem(k * 37, ndev), ndev)
            pltpu.make_async_remote_copy(
                src_ref=sendbuf.at[c, pl.ds(pl.multiple_of(peer * 8, 8), ROWS[c]), :],
                dst_ref=recvbuf.at[c, pl.ds(pl.multiple_of(me * 8, 8), ROWS[c]), :],
                send_sem=send_sem.at[c],
                recv_sem=recv_sem.at[c],
                device_id=(peer // ncol, lax.rem(peer, ncol)),
                device_id_type=MESH,
            ).start()
            return carry

        lax.fori_loop(1, ndev, one, 0)

    trace = jnp.zeros((1, LANES), jnp.float32)
    ready, a = 0, 0
    for c in range(len(ROWS)):
        need = min(c * CHUNK + CHUNK, NWORDS)
        while a < NF and SEGMENTS[a, 0, 0][0] < need:
            trace = trace + moments(a)
            a += 1
        pack(c, jnp.sum((lame + 4.0 * shear) * trace))
        if c == 0:
            pl.semaphore_wait(barrier, ndev - 1)
        send(c)

    def arrived(c):
        rows = (ndev - 1) * ROWS[c]
        pltpu.make_async_copy(
            recvbuf.at[c, pl.ds(0, rows), :], recvbuf.at[c, pl.ds(0, rows), :], recv_sem.at[c]
        ).wait()

    for c in range(len(ROWS)):
        arrived(c)
        for j in range(ROWS[c] // CAP):
            words = jnp.concatenate(
                [recvbuf[c, pl.ds(CAP * j + r, LANES, stride=8), :] for r in range(CAP)], axis=0
            )
            if c == 0 and j == 0:
                lanes = lax.broadcasted_iota(jnp.int32, (CAP * LANES, LANES), 1)
                hit = jnp.where(words[:, 0:1] - 1.0 == lanes.astype(jnp.float32), 1.0, 0.0)
                hit_t = jnp.concatenate([hit[0:LANES].T, hit[LANES:].T], axis=1)
                hit_t = hit_t.astype(jnp.bfloat16)
                place[...] = jnp.concatenate([hit_t, hit_t], axis=1)
            if c == NWORDS // CHUNK and j == NWORDS % CHUNK // LANES:
                total = jnp.sum(jnp.where(lane_iota == TRACE_LANE, words[0:LANES], 0.0))
                total_ref[...] = jnp.full(total_ref.shape, total, jnp.float32)
            out_t = jnp.dot(
                place[...], split_high_low(words, 0), preferred_element_type=jnp.float32
            )
            placed_ref[pl.ds(c * CHUNK + j * LANES, LANES), :] = out_t.T

    for c in range(len(ROWS)):
        rows = (ndev - 1) * ROWS[c]
        pltpu.make_async_copy(
            sendbuf.at[c, pl.ds(0, rows), :], sendbuf.at[c, pl.ds(0, rows), :], send_sem.at[c]
        ).wait()


def mirror_kernel(factor, placed_ref, total_ref, out_ref, planes, sems):
    inverse = factor / total_ref[0:1, :]
    copies = []
    for a in range(NF):
        for i in range(3):
            for j in range(3):
                start, skip = SEGMENTS[a, i, j]
                n, b = NF - a - skip, a + skip
                if n == 0:
                    continue
                values = placed_ref[pl.ds(start, n), :] * inverse
                planes[pl.ds((3 * a + i) * OPITCH + 3 * b + j, n, stride=3), :] = values
                planes[pl.ds((3 * b + j) * OPITCH + 3 * a + i, n, stride=3 * OPITCH), :] = values
        for i in range(3):
            m = 3 * a + i
            copy = pltpu.make_async_copy(
                planes.at[pl.ds(m * OPITCH, NDOF), :], out_ref.at[m], sems.at[m]
            )
            copy.start()
            copies.append(copy)
    for copy in copies:
        copy.wait()


def shards(nrow, ncol, grads, weights, counts, lame_first, shear, dest_owner, dest_slot):
    count = grads.shape[3]
    ndev = nrow * ncol
    vmem = pl.BlockSpec(memory_space=pltpu.VMEM)
    by_dof = jnp.transpose(grads, (1, 2, 0, 3)).reshape(NDOF, Q, count)
    placed, total = pl.pallas_call(
        functools.partial(exchange_kernel, ndev, ncol),
        out_shape=(
            jax.ShapeDtypeStruct((WORDS, LANES), jnp.float32),
            jax.ShapeDtypeStruct((8, LANES), jnp.float32),
        ),
        in_specs=[pl.BlockSpec(memory_space=pl.ANY)] + [vmem] * 6,
        out_specs=(vmem, vmem),
        scratch_shapes=[
            pltpu.VMEM((NDOF, Q, LANES), jnp.float32),
            pltpu.SemaphoreType.DMA,
            pltpu.VMEM((Q, LANES), jnp.float32),
            pltpu.VMEM((9 * 8 * PITCH + 24, LANES), jnp.float32),
            pltpu.VMEM((WORDS, LANES), jnp.float32),
            pltpu.VMEM((CAP * LANES, 2 * LANES), jnp.bfloat16),
            pltpu.VMEM((LANES, 2 * CAP * LANES), jnp.bfloat16),
            pltpu.VMEM((len(ROWS), LANES * 8 + 8, LANES), jnp.float32),
            pltpu.VMEM((len(ROWS), LANES * 8 + 8, LANES), jnp.float32),
            pltpu.SemaphoreType.DMA((len(ROWS),)),
            pltpu.SemaphoreType.DMA((len(ROWS),)),
        ],
        compiler_params=pltpu.CompilerParams(
            collective_id=0, has_side_effects=True, vmem_limit_bytes=24 << 20
        ),
    )(
        by_dof, weights, counts.reshape(1, count), lame_first.reshape(1, count),
        shear.reshape(1, count), dest_owner.reshape(1, count), dest_slot.reshape(1, count),
    )
    return pl.pallas_call(
        functools.partial(mirror_kernel, float(NDOF * count * ndev)),
        out_shape=jax.ShapeDtypeStruct((NDOF, NDOF, LANES), jnp.float32),
        in_specs=[vmem, vmem],
        out_specs=pl.BlockSpec(memory_space=pl.ANY),
        scratch_shapes=[
            pltpu.VMEM(((NDOF + 3) * OPITCH, LANES), jnp.float32),
            pltpu.SemaphoreType.DMA((NDOF,)),
        ],
        compiler_params=pltpu.CompilerParams(vmem_limit_bytes=16 << 20),
    )(placed, total)


def solution(mesh):
    axes = ("row", "col")
    return jax.shard_map(
        functools.partial(shards, mesh.shape["row"], mesh.shape["col"]),
        mesh=mesh,
        in_specs=(
            P(None, None, None, axes),
            P(None, axes),
            P(axes),
            P(axes),
            P(axes),
            P(axes, None),
            P(axes),
        ),
        out_specs=P(None, None, axes),
        check_vma=False,
    )
```

time: 140 us -> 44.2 us (0.32)
  blocking collectives: 49.2 us -> 0 us
  local copies, waits for them, and re-layouts: 44.9 us -> 5.58 us
  Pallas kernels: 0 us -> 38.3 us
  starting transfers between devices: 21.2 us -> 0 us
  matrix products: 16.2 us -> 0 us
  other arithmetic: 7.21 us -> 0 us
    psum x4 -> x0, blocking collectives: 49.2 us -> none  [one_axis_at_a_time(): return functools.reduce(lax.psum, axes, value)]
    pallas_call x0 -> x2, Pallas kernels: none -> 38.3 us  [the longest x1 36.6 us: shards(): pl.pallas_call(functools.partial(exchange_kernel, ndev, ncol), out_shape=...]
    all_to_all x2 -> x0, starting transfers between devices: 21.2 us -> none  [the longest x1 11.5 us: deliver(): lax.all_to_all(slotcol, ROW_COL, split_axis=1, concat_axis=1, tiled=True)]
    dot_general x2 -> x0, matrix products: 16.2 us -> none  [the longest x1 12.3 us: stiffness(): jnp.einsum('qme,qne->mne', gflat * weff[:, None, :], gflat, precision=lax...]
    gather x3 -> x0, local copies, waits for them, and re-layouts: 14.7 us -> none  [the longest x1 9.98 us: shards(): received = jnp.take(moved, jnp.asarray(mirror_index, jnp.int32), axis=0)]
    reshape x4 -> x0, local copies, waits for them, and re-layouts: 11.9 us -> none  [the longest x1 4.68 us: shards(): gflat = grads.reshape(Q, NDOF, count)]
    all_to_all x4 -> x0, local copies, waits for them, and re-layouts: 7.67 us -> none  [the longest x3 6.9 us: deliver(): lax.all_to_all(payload, ROW_COL, split_axis=1, concat_axis=1, tiled=True)]
    unnamed x14, local copies, waits for them, and re-layouts: 0.27 us -> 5.58 us
  transfers between devices with their start and end apart: 2 -> 0, of which waited for: 0 -> 0; matrix products, arithmetic and copies ran while one was open for 29% -> 0% of each run, Pallas kernels for 0% -> 0%
where the time goes in v1:
time: 44.2 us; the launch traced here: 43.9 us
  Pallas kernels  38.3 us (87%)
  local copies, waits for them, and re-layouts  5.58 us (13%)
    pallas_call x1, Pallas kernels, shards(): pl.pallas_call(functools.partial(exchange_kernel, ndev, ncol), out_shape=...  36.6 us
    unnamed x14, local copies, waits for them, and re-layouts  5.58 us
    pallas_call x1, Pallas kernels, shards(): pl.pallas_call(functools.partial(mirror_kernel, float(NDOF * count * ndev...  1.78 us

profile of v1, /device:TPU:1, one launch (start us, length us, event | category | flops | bytes accessed | tf_op | source)
XLA Modules:
  0.0 43.9 jit_solution(12417770819532478239)
XLA Ops:
  0.0 0.0 copy-start
  0.0 1.5 %copy-done = f32[64,20,3,128]{3,0,2,1:T(8,128)S(1)} copy-done((f32[64,20,3,128]{3,0,2,1:T(8,128)S(1)}, f32[64,20,3,128]{3,0,2,1:T(8,128)}, u32[]{:S(2)}) %copy-start) | copy-done | bytes 1966104
  1.5 0.0 copy-start.1
  1.5 0.8 %copy-done.1 = f32[64,128]{1,0:T(8,128)S(1)} copy-done((f32[64,128]{1,0:T(8,128)S(1)}, f32[64,128]{1,0:T(8,128)}, u32[]{:S(2)}) %copy-start.1) | copy-done | bytes 32792
  2.3 0.0 copy-start.2
  2.3 0.7 %copy-done.2 = s32[128]{0:T(128)S(1)} copy-done((s32[128]{0:T(128)S(1)}, s32[128]{0:T(128)}, u32[]{:S(2)}) %copy-start.2) | copy-done | bytes 536
  3.0 0.0 copy-start.3
  3.0 0.7 %copy-done.3 = f32[128]{0:T(128)S(1)} copy-done((f32[128]{0:T(128)S(1)}, f32[128]{0:T(128)}, u32[]{:S(2)}) %copy-start.3) | copy-done | bytes 536
  3.6 0.0 copy-start.4
  3.6 0.7 %copy-done.4 = f32[128]{0:T(128)S(1)} copy-done((f32[128]{0:T(128)S(1)}, f32[128]{0:T(128)}, u32[]{:S(2)}) %copy-start.4) | copy-done | bytes 536
  4.3 0.0 copy-start.5
  4.3 0.7 %copy-done.5 = s32[128,1]{0,1:T(1,128)S(1)} copy-done((s32[128,1]{0,1:T(1,128)S(1)}, s32[128,1]{0,1:T(1,128)}, u32[]{:S(2)}) %copy-start.5) | copy-done | bytes 536
  4.9 0.0 copy-start.6
  4.9 0.7 %copy-done.6 = s32[128]{0:T(128)S(1)} copy-done((s32[128]{0:T(128)S(1)}, s32[128]{0:T(128)}, u32[]{:S(2)}) %copy-start.6) | copy-done | bytes 536
  5.6 36.6 %shard_map.73 = (f32[1920,128]{1,0:T(8,128)S(1)}, f32[8,128]{1,0:T(8,128)S(1)}) custom-call(f32[60,64,128]{2,1,0:T(8,128)S(1)} %bitcast.8, f32[64,128]{1,0:T(8,128)S(1)} %copy-done.1, s32[1,128]{1,0:T(1,128)S(1)} %bitcast.9, f32[1,128]{1,0:T(1,128)S(1)} %bitcast.10, f32[1,128]{1,0:T(1,128)S(1)} %bitcast.11, s32[1,128]{1,0:T(1,128)S(1)} %bitcast.12, ...), custom_call_target="tpu_custom_call" | custom-call | tf_op jit(solution)/shard_map/pallas_call | solution.py:234
  42.2 1.8 %shard_map.74 = f32[60,60,128]{2,1,0:T(8,128)} custom-call(f32[1920,128]{1,0:T(8,128)S(1)} %get-tuple-element.7.placed_ref, f32[8,128]{1,0:T(8,128)S(1)} %get-tuple-element.8.total_ref), custom_call_target="tpu_custom_call" | custom-call | tf_op jit(solution)/shard_map/pallas_call | solution.py:262
Async XLA Ops:
  0.0 1.5 %copy-start = (f32[64,20,3,128]{3,0,2,1:T(8,128)S(1)}, f32[64,20,3,128]{3,0,2,1:T(8,128)}, u32[]{:S(2)}) copy-start(f32[64,20,3,128]{3,0,2,1:T(8,128)} %param.7) | copy-start | bytes 5898244
  1.5 0.8 %copy-start.1 = (f32[64,128]{1,0:T(8,128)S(1)}, f32[64,128]{1,0:T(8,128)}, u32[]{:S(2)}) copy-start(f32[64,128]{1,0:T(8,128)} %weights_ref.1) | copy-start | bytes 98308
  2.3 0.7 %copy-start.2 = (s32[128]{0:T(128)S(1)}, s32[128]{0:T(128)}, u32[]{:S(2)}) copy-start(s32[128]{0:T(128)} %param.9) | copy-start | bytes 1540
  3.0 0.7 %copy-start.3 = (f32[128]{0:T(128)S(1)}, f32[128]{0:T(128)}, u32[]{:S(2)}) copy-start(f32[128]{0:T(128)} %param.10) | copy-start | bytes 1540
  3.6 0.7 %copy-start.4 = (f32[128]{0:T(128)S(1)}, f32[128]{0:T(128)}, u32[]{:S(2)}) copy-start(f32[128]{0:T(128)} %param.11) | copy-start | bytes 1540
  4.3 0.7 %copy-start.5 = (s32[128,1]{0,1:T(1,128)S(1)}, s32[128,1]{0,1:T(1,128)}, u32[]{:S(2)}) copy-start(s32[128,1]{0,1:T(1,128)} %param.12) | copy-start | bytes 1540
  4.9 0.7 %copy-start.6 = (s32[128]{0:T(128)S(1)}, s32[128]{0:T(128)}, u32[]{:S(2)}) copy-start(s32[128]{0:T(128)} %param.13) | copy-start | bytes 1540

commit v2 on v1

--- a/solution.py
+++ b/solution.py
@@ -44,12 +44,23 @@
 
 def exchange_kernel(
     ndev, ncol,
-    grads_ref, weights_ref, counts_ref, lame_ref, shear_ref, owner_ref, slot_ref,
+    grads_hbm, weights_hbm, counts_hbm, lame_hbm, shear_hbm, owner_hbm, slot_hbm,
     placed_ref, total_ref,
-    gbuf, gsem, weff, partial, kmat, permute, place, sendbuf, recvbuf, send_sem, recv_sem,
+    gbuf, weights_ref, counts_ref, lame_ref, shear_ref, owner_ref, slot_ref, load_sems, weff, partial, kmat, permute, place, sendbuf, recvbuf, send_sem, recv_sem,
 ):
     row, col = lax.axis_index("row"), lax.axis_index("col")
     me = row * ncol + col
+
+    loads = [
+        pltpu.make_async_copy(source, target, load_sems.at[k])
+        for k, (source, target) in enumerate((
+            (owner_hbm, owner_ref), (counts_hbm, counts_ref), (lame_hbm, lame_ref),
+            (shear_hbm, shear_ref), (slot_hbm, slot_ref), (weights_hbm, weights_ref),
+            (grads_hbm, gbuf),
+        ))
+    ]
+    for load in loads:
+        load.start()
 
     barrier = pltpu.get_barrier_semaphore()
 
@@ -62,8 +73,8 @@
 
     lax.fori_loop(1, ndev, greet, 0)
 
-    load = pltpu.make_async_copy(grads_ref, gbuf, gsem)
-    load.start()
+    for load in loads[:-1]:
+        load.wait()
 
     owner = owner_ref[...].astype(jnp.float32)
     wide = jnp.broadcast_to(owner, (LANES, LANES))
@@ -86,7 +97,7 @@
     kmat[pl.ds(0, 1), :] = slot_ref[...].astype(jnp.float32) + 1.0
     kmat[pl.ds(NWORDS, WORDS - NWORDS), :] = jnp.zeros((WORDS - NWORDS, LANES), jnp.float32)
 
-    load.wait()
+    loads[-1].wait()
 
     def moments(a):
         gw = [
@@ -237,11 +248,17 @@
             jax.ShapeDtypeStruct((WORDS, LANES), jnp.float32),
             jax.ShapeDtypeStruct((8, LANES), jnp.float32),
         ),
-        in_specs=[pl.BlockSpec(memory_space=pl.ANY)] + [vmem] * 6,
+        in_specs=[pl.BlockSpec(memory_space=pltpu.HBM)] * 7,
         out_specs=(vmem, vmem),
         scratch_shapes=[
             pltpu.VMEM((NDOF, Q, LANES), jnp.float32),
-            pltpu.SemaphoreType.DMA,
+            pltpu.VMEM((Q, LANES), jnp.float32),
+            pltpu.VMEM((1, LANES), jnp.int32),
+            pltpu.VMEM((1, LANES), jnp.float32),
+            pltpu.VMEM((1, LANES), jnp.float32),
+            pltpu.VMEM((1, LANES), jnp.int32),
+            pltpu.VMEM((1, LANES), jnp.int32),
+            pltpu.SemaphoreType.DMA((7,)),
             pltpu.VMEM((Q, LANES), jnp.float32),
             pltpu.VMEM((9 * 8 * PITCH + 24, LANES), jnp.float32),
             pltpu.VMEM((WORDS, LANES), jnp.float32),

time: 44.2 us -> 44.7 us (1.011)
  Pallas kernels: 38.3 us -> 38.9 us
    pallas_call x1, Pallas kernels: 36.6 us -> 37.1 us  [shards(): pl.pallas_call(functools.partial(exchange_kernel, ndev, ncol), out_shape=...]
where the time goes in v2:
time: 44.7 us; the launch traced here: 44.5 us
  Pallas kernels  38.9 us (87%)
  local copies, waits for them, and re-layouts  5.58 us (12%)
    pallas_call x1, Pallas kernels, shards(): pl.pallas_call(functools.partial(exchange_kernel, ndev, ncol), out_shape=...  37.1 us
    unnamed x14, local copies, waits for them, and re-layouts  5.58 us
    pallas_call x1, Pallas kernels, shards(): pl.pallas_call(functools.partial(mirror_kernel, float(NDOF * count * ndev...  1.78 us

profile of v2, /device:TPU:1, one launch (start us, length us, event | category | flops | bytes accessed | tf_op | source)
XLA Modules:
  0.0 44.5 jit_solution(1302766086794134653)
XLA Ops:
  0.0 0.0 copy-start
  0.0 1.5 %copy-done = f32[64,20,3,128]{3,0,2,1:T(8,128)S(1)} copy-done((f32[64,20,3,128]{3,0,2,1:T(8,128)S(1)}, f32[64,20,3,128]{3,0,2,1:T(8,128)}, u32[]{:S(2)}) %copy-start) | copy-done | bytes 1966104
  1.5 0.0 copy-start.1
  1.5 0.8 %copy-done.1 = f32[64,128]{1,0:T(8,128)S(1)} copy-done((f32[64,128]{1,0:T(8,128)S(1)}, f32[64,128]{1,0:T(8,128)}, u32[]{:S(2)}) %copy-start.1) | copy-done | bytes 32792
  2.3 0.0 copy-start.2
  2.3 0.7 %copy-done.2 = s32[128]{0:T(128)S(1)} copy-done((s32[128]{0:T(128)S(1)}, s32[128]{0:T(128)}, u32[]{:S(2)}) %copy-start.2) | copy-done | bytes 536
  3.0 0.0 copy-start.3
  3.0 0.7 %copy-done.3 = f32[128]{0:T(128)S(1)} copy-done((f32[128]{0:T(128)S(1)}, f32[128]{0:T(128)}, u32[]{:S(2)}) %copy-start.3) | copy-done | bytes 536
  3.6 0.0 copy-start.4
  3.6 0.7 %copy-done.4 = f32[128]{0:T(128)S(1)} copy-done((f32[128]{0:T(128)S(1)}, f32[128]{0:T(128)}, u32[]{:S(2)}) %copy-start.4) | copy-done | bytes 536
  4.3 0.0 copy-start.5
  4.3 0.7 %copy-done.5 = s32[128,1]{0,1:T(1,128)S(1)} copy-done((s32[128,1]{0,1:T(1,128)S(1)}, s32[128,1]{0,1:T(1,128)}, u32[]{:S(2)}) %copy-start.5) | copy-done | bytes 536
  4.9 0.0 copy-start.6
  4.9 0.7 %copy-done.6 = s32[128]{0:T(128)S(1)} copy-done((s32[128]{0:T(128)S(1)}, s32[128]{0:T(128)}, u32[]{:S(2)}) %copy-start.6) | copy-done | bytes 536
  5.6 37.1 %shard_map.73 = (f32[1920,128]{1,0:T(8,128)S(1)}, f32[8,128]{1,0:T(8,128)S(1)}) custom-call(f32[60,64,128]{2,1,0:T(8,128)S(1)} %bitcast.8, f32[64,128]{1,0:T(8,128)S(1)} %copy-done.1, s32[1,128]{1,0:T(1,128)S(1)} %bitcast.9, f32[1,128]{1,0:T(1,128)S(1)} %bitcast.10, f32[1,128]{1,0:T(1,128)S(1)} %bitcast.11, s32[1,128]{1,0:T(1,128)S(1)} %bitcast.12, ...), custom_call_target="tpu_custom_call" | custom-call | tf_op jit(solution)/shard_map/pallas_call | solution.py:245
  42.7 1.8 %shard_map.74 = f32[60,60,128]{2,1,0:T(8,128)} custom-call(f32[1920,128]{1,0:T(8,128)S(1)} %get-tuple-element.7.placed_ref, f32[8,128]{1,0:T(8,128)S(1)} %get-tuple-element.8.total_ref), custom_call_target="tpu_custom_call" | custom-call | tf_op jit(solution)/shard_map/pallas_call | solution.py:279
Async XLA Ops:
  0.0 1.5 %copy-start = (f32[64,20,3,128]{3,0,2,1:T(8,128)S(1)}, f32[64,20,3,128]{3,0,2,1:T(8,128)}, u32[]{:S(2)}) copy-start(f32[64,20,3,128]{3,0,2,1:T(8,128)} %param.7) | copy-start | bytes 5898244
  1.5 0.8 %copy-start.1 = (f32[64,128]{1,0:T(8,128)S(1)}, f32[64,128]{1,0:T(8,128)}, u32[]{:S(2)}) copy-start(f32[64,128]{1,0:T(8,128)} %weights_hbm.1) | copy-start | bytes 98308
  2.3 0.7 %copy-start.2 = (s32[128]{0:T(128)S(1)}, s32[128]{0:T(128)}, u32[]{:S(2)}) copy-start(s32[128]{0:T(128)} %param.9) | copy-start | bytes 1540
  3.0 0.7 %copy-start.3 = (f32[128]{0:T(128)S(1)}, f32[128]{0:T(128)}, u32[]{:S(2)}) copy-start(f32[128]{0:T(128)} %param.10) | copy-start | bytes 1540
  3.6 0.7 %copy-start.4 = (f32[128]{0:T(128)S(1)}, f32[128]{0:T(128)}, u32[]{:S(2)}) copy-start(f32[128]{0:T(128)} %param.11) | copy-start | bytes 1540
  4.3 0.7 %copy-start.5 = (s32[128,1]{0,1:T(1,128)S(1)}, s32[128,1]{0,1:T(1,128)}, u32[]{:S(2)}) copy-start(s32[128,1]{0,1:T(1,128)} %param.12) | copy-start | bytes 1540
  4.9 0.7 %copy-start.6 = (s32[128]{0:T(128)S(1)}, s32[128]{0:T(128)}, u32[]{:S(2)}) copy-start(s32[128]{0:T(128)} %param.13) | copy-start | bytes 1540

commit v3 on v2

--- a/solution.py
+++ b/solution.py
@@ -272,10 +272,13 @@
         compiler_params=pltpu.CompilerParams(
             collective_id=0, has_side_effects=True, vmem_limit_bytes=24 << 20
         ),
-    )(
-        by_dof, weights, counts.reshape(1, count), lame_first.reshape(1, count),
-        shear.reshape(1, count), dest_owner.reshape(1, count), dest_slot.reshape(1, count),
-    )
+    )(*(
+        pltpu.with_memory_space_constraint(operand, pltpu.HBM)
+        for operand in (
+            by_dof, weights, counts.reshape(1, count), lame_first.reshape(1, count),
+            shear.reshape(1, count), dest_owner.reshape(1, count), dest_slot.reshape(1, count),
+        )
+    ))
     return pl.pallas_call(
         functools.partial(mirror_kernel, float(NDOF * count * ndev)),
         out_shape=jax.ShapeDtypeStruct((NDOF, NDOF, LANES), jnp.float32),

time: 44.7 us -> 38.6 us (0.86)
  local copies, waits for them, and re-layouts: 5.58 us -> 0 us
    unnamed x14 -> x0, local copies, waits for them, and re-layouts: 5.58 us -> none
where the time goes in v3:
time: 38.6 us; the launch traced here: 38.5 us
  Pallas kernels  38.5 us (100%)
    pallas_call x1, Pallas kernels, shards(): pl.pallas_call(functools.partial(exchange_kernel, ndev, ncol), out_shape=...  36.7 us
    pallas_call x1, Pallas kernels, shards(): pl.pallas_call(functools.partial(mirror_kernel, float(NDOF * count * ndev...  1.78 us

profile of v3, /device:TPU:1, one launch (start us, length us, event | category | flops | bytes accessed | tf_op | source)
XLA Modules:
  0.0 38.5 jit_solution(8971317389469360358)
XLA Ops:
  0.0 36.7 %shard_map.73 = (f32[1920,128]{1,0:T(8,128)S(1)}, f32[8,128]{1,0:T(8,128)S(1)}) custom-call(f32[60,64,128]{2,1,0:T(8,128)} %bitcast.8, f32[64,128]{1,0:T(8,128)} %weights_hbm.1, s32[1,128]{1,0:T(1,128)} %bitcast.9, f32[1,128]{1,0:T(1,128)} %bitcast.10, f32[1,128]{1,0:T(1,128)} %bitcast.11, s32[1,128]{1,0:T(1,128)} %bitcast.12, s32[1,128]{1,0:T(1,128)} %bitcast.13), custom_call_target="tpu_custom_call" | custom-call | tf_op jit(solution)/shard_map/pallas_call | solution.py:245
  36.7 1.8 %shard_map.74 = f32[60,60,128]{2,1,0:T(8,128)} custom-call(f32[1920,128]{1,0:T(8,128)S(1)} %get-tuple-element.7.placed_ref, f32[8,128]{1,0:T(8,128)S(1)} %get-tuple-element.8.total_ref), custom_call_target="tpu_custom_call" | custom-call | tf_op jit(solution)/shard_map/pallas_call | solution.py:282

commit v4 on v3

--- a/solution.py
+++ b/solution.py
@@ -14,14 +14,14 @@
 LANES = 128
 CAP = 2
 CHUNK = 512
-ROWS = (8, 8, 8, 6)
+ROWS = (8, 8, 8, 5)
 PITCH = 20
 OPITCH = 72
 MESH = pl.DeviceIdType.MESH
 
 
 def segments():
-    table, row = {}, 1
+    table, row = {}, 2
     for a in range(NF):
         for i in range(3):
             for j in range(3):
@@ -32,8 +32,8 @@
 
 
 SEGMENTS, NWORDS = segments()
-WORDS = 64 * CAP * 15
-TRACE_LANE = NWORDS % LANES
+WORDS = 15 * LANES
+HALF = LANES // 2
 
 
 def split_high_low(x, axis):
@@ -43,13 +43,14 @@
 
 
 def exchange_kernel(
-    ndev, ncol,
+    nrow, ncol,
     grads_hbm, weights_hbm, counts_hbm, lame_hbm, shear_hbm, owner_hbm, slot_hbm,
-    placed_ref, total_ref,
-    gbuf, weights_ref, counts_ref, lame_ref, shear_ref, owner_ref, slot_ref, load_sems, weff, partial, kmat, permute, place, sendbuf, recvbuf, send_sem, recv_sem,
+    planes_ref,
+    gbuf, weights_ref, counts_ref, lame_ref, shear_ref, owner_ref, slot_ref, load_sems, weff, partial, kmat, placed, permute, place, sendbuf, recvbuf, send_sem, recv_sem,
 ):
     row, col = lax.axis_index("row"), lax.axis_index("col")
     me = row * ncol + col
+    ndev = nrow * ncol
 
     loads = [
         pltpu.make_async_copy(source, target, load_sems.at[k])
@@ -64,14 +65,14 @@
 
     barrier = pltpu.get_barrier_semaphore()
 
-    def greet(k, carry):
-        peer = lax.rem(me + k, ndev)
-        pl.semaphore_signal(
-            barrier, inc=1, device_id=(peer // ncol, lax.rem(peer, ncol)), device_id_type=MESH
-        )
-        return carry
-
-    lax.fori_loop(1, ndev, greet, 0)
+    rows_at = [lax.rem(row + k, nrow) for k in range(nrow)]
+    cols_at = [lax.rem(col + k, ncol) for k in range(ncol)]
+    for dr in range(nrow):
+        for dc in range(ncol):
+            if dr or dc:
+                pl.semaphore_signal(
+                    barrier, inc=1, device_id=(rows_at[dr], cols_at[dc]), device_id_type=MESH
+                )
 
     for load in loads[:-1]:
         load.wait()
@@ -136,46 +137,61 @@
                     continue
                 k = lame * m[i][j] + shear * (m[j][i] + across if i == j else m[j][i])
                 kmat[pl.ds(start, n - skip), :] = k[skip:]
-        return across[0:1]
-
-    def pack(c, local_total):
-        for j in range(ROWS[c] // CAP):
+
+    def pack(c):
+        for j in range((ROWS[c] + 1) // CAP):
             words = kmat[pl.ds(c * CHUNK + j * LANES, LANES), :]
             out = lax.dot_general(
                 permute[...], split_high_low(words, 1), (((1,), (1,)), ((), ())),
                 preferred_element_type=jnp.float32,
             )
-            for r in range(CAP):
-                part = out[r * LANES:(r + 1) * LANES]
-                if r == 0 and c == NWORDS // CHUNK and j == NWORDS % CHUNK // LANES:
-                    part = jnp.where(lane_iota == TRACE_LANE, local_total, part)
+            parts = [out[r * LANES:(r + 1) * LANES] for r in range(CAP)]
+            if c == 0 and j == 0:
+                parts[0] = jnp.where(lane_iota == 1, local_trace, parts[0])
+            if CAP * (j + 1) > ROWS[c]:
+                parts = [parts[0] + pltpu.roll(parts[1], HALF, 1)]
+            for r, part in enumerate(parts):
                 sendbuf[c, pl.ds(CAP * j + r, LANES, stride=8), :] = part
         own = pl.multiple_of(me * 8, 8)
         recvbuf[c, pl.ds(own, 8), :] = sendbuf[c, pl.ds(own, 8), :]
 
     def send(c):
-        def one(k, carry):
-            peer = lax.rem(me + lax.rem(k * 37, ndev), ndev)
+        def to(peer_row, dc):
+            peer = peer_row * ncol + cols_at[dc]
             pltpu.make_async_remote_copy(
                 src_ref=sendbuf.at[c, pl.ds(pl.multiple_of(peer * 8, 8), ROWS[c]), :],
                 dst_ref=recvbuf.at[c, pl.ds(pl.multiple_of(me * 8, 8), ROWS[c]), :],
                 send_sem=send_sem.at[c],
                 recv_sem=recv_sem.at[c],
-                device_id=(peer // ncol, lax.rem(peer, ncol)),
+                device_id=(peer_row, cols_at[dc]),
                 device_id_type=MESH,
             ).start()
+
+        def to_row(dr, carry):
+            peer_row = lax.rem(row + dr, nrow)
+            for dc in range(ncol):
+                to(peer_row, dc)
             return carry
 
-        lax.fori_loop(1, ndev, one, 0)
-
-    trace = jnp.zeros((1, LANES), jnp.float32)
-    ready, a = 0, 0
+        lax.fori_loop(1, nrow, to_row, 0)
+        for dc in range(1, ncol):
+            to(row, dc)
+
+    squares = [jnp.zeros((8, LANES), jnp.float32)] * NQB
+    for m in range(NDOF):
+        for qb in range(NQB):
+            g = gbuf[m, pl.ds(8 * qb, 8), :]
+            squares[qb] = squares[qb] + g * g
+    weighted = sum(weff[pl.ds(8 * qb, 8), :] * squares[qb] for qb in range(NQB))
+    local_trace = jnp.sum((lame + 4.0 * shear) * weighted)
+
+    a = 0
     for c in range(len(ROWS)):
         need = min(c * CHUNK + CHUNK, NWORDS)
         while a < NF and SEGMENTS[a, 0, 0][0] < need:
-            trace = trace + moments(a)
+            moments(a)
             a += 1
-        pack(c, jnp.sum((lame + 4.0 * shear) * trace))
+        pack(c)
         if c == 0:
             pl.semaphore_wait(barrier, ndev - 1)
         send(c)
@@ -186,25 +202,39 @@
             recvbuf.at[c, pl.ds(0, rows), :], recvbuf.at[c, pl.ds(0, rows), :], recv_sem.at[c]
         ).wait()
 
+    inverse = None
+    pending = [key for key in SEGMENTS if NF - key[0] > SEGMENTS[key][1]]
     for c in range(len(ROWS)):
         arrived(c)
-        for j in range(ROWS[c] // CAP):
-            words = jnp.concatenate(
-                [recvbuf[c, pl.ds(CAP * j + r, LANES, stride=8), :] for r in range(CAP)], axis=0
-            )
+        for j in range((ROWS[c] + 1) // CAP):
+            if CAP * (j + 1) > ROWS[c]:
+                shared = recvbuf[c, pl.ds(CAP * j, LANES, stride=8), :]
+                parts = [shared, pltpu.roll(shared, HALF, 1)]
+            else:
+                parts = [recvbuf[c, pl.ds(CAP * j + r, LANES, stride=8), :] for r in range(CAP)]
+            words = jnp.concatenate(parts, axis=0)
             if c == 0 and j == 0:
                 lanes = lax.broadcasted_iota(jnp.int32, (CAP * LANES, LANES), 1)
                 hit = jnp.where(words[:, 0:1] - 1.0 == lanes.astype(jnp.float32), 1.0, 0.0)
                 hit_t = jnp.concatenate([hit[0:LANES].T, hit[LANES:].T], axis=1)
                 hit_t = hit_t.astype(jnp.bfloat16)
                 place[...] = jnp.concatenate([hit_t, hit_t], axis=1)
-            if c == NWORDS // CHUNK and j == NWORDS % CHUNK // LANES:
-                total = jnp.sum(jnp.where(lane_iota == TRACE_LANE, words[0:LANES], 0.0))
-                total_ref[...] = jnp.full(total_ref.shape, total, jnp.float32)
+                total = jnp.sum(parts[0][:, 1:2], axis=0, keepdims=True)
+                inverse = jnp.broadcast_to(float(NDOF * LANES * ndev) / total, (8, LANES))
             out_t = jnp.dot(
                 place[...], split_high_low(words, 0), preferred_element_type=jnp.float32
             )
-            placed_ref[pl.ds(c * CHUNK + j * LANES, LANES), :] = out_t.T
+            placed[pl.ds(c * CHUNK + j * LANES, LANES), :] = out_t.T
+        while pending:
+            a, i, j = pending[0]
+            start, skip = SEGMENTS[a, i, j]
+            n, b = NF - a - skip, a + skip
+            if c < len(ROWS) - 1 and start + n > (c + 1) * CHUNK:
+                break
+            pending.pop(0)
+            values = placed[pl.ds(start, n), :] * inverse[0:1]
+            planes_ref[pl.ds((3 * a + i) * OPITCH + 3 * b + j, n, stride=3), :] = values
+            planes_ref[pl.ds((3 * b + j) * OPITCH + 3 * a + i, n, stride=3 * OPITCH), :] = values
 
     for c in range(len(ROWS)):
         rows = (ndev - 1) * ROWS[c]
@@ -213,43 +243,28 @@
         ).wait()
 
 
-def mirror_kernel(factor, placed_ref, total_ref, out_ref, planes, sems):
-    inverse = factor / total_ref[0:1, :]
-    copies = []
-    for a in range(NF):
-        for i in range(3):
-            for j in range(3):
-                start, skip = SEGMENTS[a, i, j]
-                n, b = NF - a - skip, a + skip
-                if n == 0:
-                    continue
-                values = placed_ref[pl.ds(start, n), :] * inverse
-                planes[pl.ds((3 * a + i) * OPITCH + 3 * b + j, n, stride=3), :] = values
-                planes[pl.ds((3 * b + j) * OPITCH + 3 * a + i, n, stride=3 * OPITCH), :] = values
-        for i in range(3):
-            m = 3 * a + i
-            copy = pltpu.make_async_copy(
-                planes.at[pl.ds(m * OPITCH, NDOF), :], out_ref.at[m], sems.at[m]
-            )
-            copy.start()
-            copies.append(copy)
+def copy_out_kernel(planes_ref, out_ref, sems):
+    copies = [
+        pltpu.make_async_copy(
+            planes_ref.at[pl.ds(m * OPITCH, NDOF), :], out_ref.at[m], sems.at[m]
+        )
+        for m in range(NDOF)
+    ]
+    for copy in copies:
+        copy.start()
     for copy in copies:
         copy.wait()
 
 
 def shards(nrow, ncol, grads, weights, counts, lame_first, shear, dest_owner, dest_slot):
     count = grads.shape[3]
-    ndev = nrow * ncol
     vmem = pl.BlockSpec(memory_space=pltpu.VMEM)
     by_dof = jnp.transpose(grads, (1, 2, 0, 3)).reshape(NDOF, Q, count)
-    placed, total = pl.pallas_call(
-        functools.partial(exchange_kernel, ndev, ncol),
-        out_shape=(
-            jax.ShapeDtypeStruct((WORDS, LANES), jnp.float32),
-            jax.ShapeDtypeStruct((8, LANES), jnp.float32),
-        ),
+    planes = pl.pallas_call(
+        functools.partial(exchange_kernel, nrow, ncol),
+        out_shape=jax.ShapeDtypeStruct(((NDOF + 4) * OPITCH, LANES), jnp.float32),
         in_specs=[pl.BlockSpec(memory_space=pltpu.HBM)] * 7,
-        out_specs=(vmem, vmem),
+        out_specs=vmem,
         scratch_shapes=[
             pltpu.VMEM((NDOF, Q, LANES), jnp.float32),
             pltpu.VMEM((Q, LANES), jnp.float32),
@@ -261,6 +276,7 @@
             pltpu.SemaphoreType.DMA((7,)),
             pltpu.VMEM((Q, LANES), jnp.float32),
             pltpu.VMEM((9 * 8 * PITCH + 24, LANES), jnp.float32),
+            pltpu.VMEM((WORDS, LANES), jnp.float32),
             pltpu.VMEM((WORDS, LANES), jnp.float32),
             pltpu.VMEM((CAP * LANES, 2 * LANES), jnp.bfloat16),
             pltpu.VMEM((LANES, 2 * CAP * LANES), jnp.bfloat16),
@@ -280,16 +296,13 @@
         )
     ))
     return pl.pallas_call(
-        functools.partial(mirror_kernel, float(NDOF * count * ndev)),
+        copy_out_kernel,
         out_shape=jax.ShapeDtypeStruct((NDOF, NDOF, LANES), jnp.float32),
-        in_specs=[vmem, vmem],
+        in_specs=[vmem],
         out_specs=pl.BlockSpec(memory_space=pl.ANY),
-        scratch_shapes=[
-            pltpu.VMEM(((NDOF + 3) * OPITCH, LANES), jnp.float32),
-            pltpu.SemaphoreType.DMA((NDOF,)),
-        ],
+        scratch_shapes=[pltpu.SemaphoreType.DMA((NDOF,))],
         compiler_params=pltpu.CompilerParams(vmem_limit_bytes=16 << 20),
-    )(placed, total)
+    )(planes)
 
 
 def solution(mesh):

time: 38.6 us -> 36.4 us (0.943)
  Pallas kernels: 38.5 us -> 36.2 us
    pallas_call x2, Pallas kernels: 38.5 us -> 36.2 us  [the longest x1 34.5 us: shards(): pl.pallas_call(functools.partial(exchange_kernel, nrow, ncol), out_shape=...]
where the time goes in v4:
time: 36.4 us; the launch traced here: 36.2 us
  Pallas kernels  36.2 us (99%)
    pallas_call x1, Pallas kernels, shards(): pl.pallas_call(functools.partial(exchange_kernel, nrow, ncol), out_shape=...  34.5 us
    pallas_call x1, Pallas kernels, shards(): pl.pallas_call(copy_out_kernel, out_shape=jax.ShapeDtypeStruct((NDOF, NDO...  1.74 us

profile of v4, /device:TPU:1, one launch (start us, length us, event | category | flops | bytes accessed | tf_op | source)
XLA Modules:
  0.0 36.2 jit_solution(16345216595831951794)
XLA Ops:
  0.0 34.5 %shard_map.73.planes_ref = f32[4608,128]{1,0:T(8,128)S(1)} custom-call(f32[60,64,128]{2,1,0:T(8,128)} %bitcast.8, f32[64,128]{1,0:T(8,128)} %weights_hbm.1, s32[1,128]{1,0:T(1,128)} %bitcast.9, f32[1,128]{1,0:T(1,128)} %bitcast.10, f32[1,128]{1,0:T(1,128)} %bitcast.11, s32[1,128]{1,0:T(1,128)} %bitcast.12, s32[1,128]{1,0:T(1,128)} %bitcast.13), custom_call_target="tpu_custom_call" | custom-call | tf_op jit(solution)/shard_map/pallas_call | solution.py:263
  34.5 1.7 %shard_map.74 = f32[60,60,128]{2,1,0:T(8,128)} custom-call(f32[4608,128]{1,0:T(8,128)S(1)} %shard_map.73.planes_ref), custom_call_target="tpu_custom_call" | custom-call | tf_op jit(solution)/shard_map/pallas_call | solution.py:298

commit v5 on v4

--- a/solution.py
+++ b/solution.py
@@ -16,8 +16,8 @@
 CHUNK = 512
 ROWS = (8, 8, 8, 5)
 PITCH = 20
-OPITCH = 72
 MESH = pl.DeviceIdType.MESH
+COL_ORDER = (4, 5, 2, 3, 6, 7, 0, 1)
 
 
 def segments():
@@ -67,12 +67,15 @@
 
     rows_at = [lax.rem(row + k, nrow) for k in range(nrow)]
     cols_at = [lax.rem(col + k, ncol) for k in range(ncol)]
-    for dr in range(nrow):
-        for dc in range(ncol):
-            if dr or dc:
-                pl.semaphore_signal(
-                    barrier, inc=1, device_id=(rows_at[dr], cols_at[dc]), device_id_type=MESH
-                )
+    hops = (0, 1, 2, 1)
+    order = sorted(
+        ((dr, dc) for dr in range(nrow) for dc in range(ncol) if dr or dc),
+        key=lambda o: -(hops[o[0] // 4] + hops[o[0] % 4] + hops[o[1] // 2]),
+    )
+    for dr, dc in order:
+        pl.semaphore_signal(
+            barrier, inc=1, device_id=(rows_at[dr], cols_at[dc]), device_id_type=MESH
+        )
 
     for load in loads[:-1]:
         load.wait()
@@ -95,6 +98,7 @@
             counts > qb, weights_ref[pl.ds(8 * qb, 8), :], 0.0
         )
     lame, shear = lame_ref[...], shear_ref[...]
+    kmat[pl.ds(0, 8), :] = jnp.zeros((8, LANES), jnp.float32)
     kmat[pl.ds(0, 1), :] = slot_ref[...].astype(jnp.float32) + 1.0
     kmat[pl.ds(NWORDS, WORDS - NWORDS), :] = jnp.zeros((WORDS - NWORDS, LANES), jnp.float32)
 
@@ -167,9 +171,9 @@
                 device_id_type=MESH,
             ).start()
 
-        def to_row(dr, carry):
-            peer_row = lax.rem(row + dr, nrow)
-            for dc in range(ncol):
+        def to_row(k, carry):
+            peer_row = lax.rem(row + k, nrow)
+            for dc in COL_ORDER:
                 to(peer_row, dc)
             return carry
 
@@ -233,8 +237,9 @@
                 break
             pending.pop(0)
             values = placed[pl.ds(start, n), :] * inverse[0:1]
-            planes_ref[pl.ds((3 * a + i) * OPITCH + 3 * b + j, n, stride=3), :] = values
-            planes_ref[pl.ds((3 * b + j) * OPITCH + 3 * a + i, n, stride=3 * OPITCH), :] = values
+            planes_ref[3 * a + i, pl.ds(3 * b + j, n, stride=3), :] = values
+            for t in range(n):
+                planes_ref[3 * (b + t) + j, pl.ds(3 * a + i, 1), :] = values[t:t + 1]
 
     for c in range(len(ROWS)):
         rows = (ndev - 1) * ROWS[c]
@@ -243,26 +248,13 @@
         ).wait()
 
 
-def copy_out_kernel(planes_ref, out_ref, sems):
-    copies = [
-        pltpu.make_async_copy(
-            planes_ref.at[pl.ds(m * OPITCH, NDOF), :], out_ref.at[m], sems.at[m]
-        )
-        for m in range(NDOF)
-    ]
-    for copy in copies:
-        copy.start()
-    for copy in copies:
-        copy.wait()
-
-
 def shards(nrow, ncol, grads, weights, counts, lame_first, shear, dest_owner, dest_slot):
     count = grads.shape[3]
     vmem = pl.BlockSpec(memory_space=pltpu.VMEM)
     by_dof = jnp.transpose(grads, (1, 2, 0, 3)).reshape(NDOF, Q, count)
-    planes = pl.pallas_call(
+    return pl.pallas_call(
         functools.partial(exchange_kernel, nrow, ncol),
-        out_shape=jax.ShapeDtypeStruct(((NDOF + 4) * OPITCH, LANES), jnp.float32),
+        out_shape=jax.ShapeDtypeStruct((NDOF, NDOF, LANES), jnp.float32),
         in_specs=[pl.BlockSpec(memory_space=pltpu.HBM)] * 7,
         out_specs=vmem,
         scratch_shapes=[
@@ -295,14 +287,6 @@
             shear.reshape(1, count), dest_owner.reshape(1, count), dest_slot.reshape(1, count),
         )
     ))
-    return pl.pallas_call(
-        copy_out_kernel,
-        out_shape=jax.ShapeDtypeStruct((NDOF, NDOF, LANES), jnp.float32),
-        in_specs=[vmem],
-        out_specs=pl.BlockSpec(memory_space=pl.ANY),
-        scratch_shapes=[pltpu.SemaphoreType.DMA((NDOF,))],
-        compiler_params=pltpu.CompilerParams(vmem_limit_bytes=16 << 20),
-    )(planes)
 
 
 def solution(mesh):

time: 36.4 us -> 35.8 us (0.984)
  Pallas kernels: 36.2 us -> 34.4 us
  local copies, waits for them, and re-layouts: 0 us -> 1.27 us
    pallas_call x1 -> x0, Pallas kernels: 1.74 us -> none  [shards(): pl.pallas_call(copy_out_kernel, out_shape=jax.ShapeDtypeStruct((NDOF, NDO...]
    unnamed x0 -> x1, local copies, waits for them, and re-layouts: none -> 1.27 us
where the time goes in v5:
time: 35.8 us; the launch traced here: 35.7 us
  Pallas kernels  34.4 us (96%)
  local copies, waits for them, and re-layouts  1.27 us (4%)
    pallas_call x1, Pallas kernels, shards(): pl.pallas_call(functools.partial(exchange_kernel, nrow, ncol), out_shape=...  34.4 us
    unnamed x1, local copies, waits for them, and re-layouts  1.27 us

profile of v5, /device:TPU:1, one launch (start us, length us, event | category | flops | bytes accessed | tf_op | source)
XLA Modules:
  0.0 35.7 jit_solution(5574155894973649525)
XLA Ops:
  0.0 34.4 %shard_map.73 = f32[60,60,128]{2,1,0:T(8,128)S(1)} custom-call(f32[60,64,128]{2,1,0:T(8,128)} %bitcast.8, f32[64,128]{1,0:T(8,128)} %weights_hbm.1, s32[1,128]{1,0:T(1,128)} %bitcast.9, f32[1,128]{1,0:T(1,128)} %bitcast.10, f32[1,128]{1,0:T(1,128)} %bitcast.11, s32[1,128]{1,0:T(1,128)} %bitcast.12, s32[1,128]{1,0:T(1,128)} %bitcast.13), custom_call_target="tpu_custom_call" | custom-call | tf_op jit(solution)/shard_map/pallas_call | solution.py:255
  34.4 1.3 %copy.9 = f32[60,60,128]{2,1,0:T(8,128)} copy(f32[60,60,128]{2,1,0:T(8,128)S(1)} %shard_map.73) | data formatting | bytes 3686400

commit v6 on v5

--- a/solution.py
+++ b/solution.py
@@ -13,8 +13,8 @@
 NQB = 8
 LANES = 128
 CAP = 2
-CHUNK = 512
-ROWS = (8, 8, 8, 5)
+ROWS = (6, 6, 6, 6, 5)
+STARTS = tuple(LANES * (sum(ROWS[:c]) // CAP) for c in range(len(ROWS)))
 PITCH = 20
 MESH = pl.DeviceIdType.MESH
 COL_ORDER = (4, 5, 2, 3, 6, 7, 0, 1)
@@ -144,7 +144,7 @@
 
     def pack(c):
         for j in range((ROWS[c] + 1) // CAP):
-            words = kmat[pl.ds(c * CHUNK + j * LANES, LANES), :]
+            words = kmat[pl.ds(STARTS[c] + j * LANES, LANES), :]
             out = lax.dot_general(
                 permute[...], split_high_low(words, 1), (((1,), (1,)), ((), ())),
                 preferred_element_type=jnp.float32,
@@ -191,7 +191,7 @@
 
     a = 0
     for c in range(len(ROWS)):
-        need = min(c * CHUNK + CHUNK, NWORDS)
+        need = min((STARTS + (NWORDS,))[c + 1], NWORDS)
         while a < NF and SEGMENTS[a, 0, 0][0] < need:
             moments(a)
             a += 1
@@ -228,12 +228,12 @@
             out_t = jnp.dot(
                 place[...], split_high_low(words, 0), preferred_element_type=jnp.float32
             )
-            placed[pl.ds(c * CHUNK + j * LANES, LANES), :] = out_t.T
+            placed[pl.ds(STARTS[c] + j * LANES, LANES), :] = out_t.T
         while pending:
             a, i, j = pending[0]
             start, skip = SEGMENTS[a, i, j]
             n, b = NF - a - skip, a + skip
-            if c < len(ROWS) - 1 and start + n > (c + 1) * CHUNK:
+            if c < len(ROWS) - 1 and start + n > STARTS[c + 1]:
                 break
             pending.pop(0)
             values = placed[pl.ds(start, n), :] * inverse[0:1]

time: 35.8 us -> 35.6 us (level)
  no operation moved by 1% of the time
where the time goes in v6:
time: 35.6 us; the launch traced here: 35.5 us
  Pallas kernels  34.2 us (96%)
  local copies, waits for them, and re-layouts  1.27 us (4%)
    pallas_call x1, Pallas kernels, shards(): pl.pallas_call(functools.partial(exchange_kernel, nrow, ncol), out_shape=...  34.2 us
    unnamed x1, local copies, waits for them, and re-layouts  1.27 us

profile of v6, /device:TPU:1, one launch (start us, length us, event | category | flops | bytes accessed | tf_op | source)
XLA Modules:
  0.0 35.5 jit_solution(1590410171885080218)
XLA Ops:
  0.0 34.2 %shard_map.73 = f32[60,60,128]{2,1,0:T(8,128)S(1)} custom-call(f32[60,64,128]{2,1,0:T(8,128)} %bitcast.8, f32[64,128]{1,0:T(8,128)} %weights_hbm.1, s32[1,128]{1,0:T(1,128)} %bitcast.9, f32[1,128]{1,0:T(1,128)} %bitcast.10, f32[1,128]{1,0:T(1,128)} %bitcast.11, s32[1,128]{1,0:T(1,128)} %bitcast.12, s32[1,128]{1,0:T(1,128)} %bitcast.13), custom_call_target="tpu_custom_call" | custom-call | tf_op jit(solution)/shard_map/pallas_call | solution.py:255
  34.2 1.3 %copy.9 = f32[60,60,128]{2,1,0:T(8,128)} copy(f32[60,60,128]{2,1,0:T(8,128)S(1)} %shard_map.73) | data formatting | bytes 3686400

commit v7 on v6

--- a/solution.py
+++ b/solution.py
@@ -13,7 +13,7 @@
 NQB = 8
 LANES = 128
 CAP = 2
-ROWS = (6, 6, 6, 6, 5)
+ROWS = (4, 6, 6, 6, 7)
 STARTS = tuple(LANES * (sum(ROWS[:c]) // CAP) for c in range(len(ROWS)))
 PITCH = 20
 MESH = pl.DeviceIdType.MESH

time: 35.6 us -> 35.6 us (level)
  no operation moved by 1% of the time
where the time goes in v7:
time: 35.6 us; the launch traced here: 35.4 us
  Pallas kernels  34.1 us (96%)
  local copies, waits for them, and re-layouts  1.27 us (4%)
    pallas_call x1, Pallas kernels, shards(): pl.pallas_call(functools.partial(exchange_kernel, nrow, ncol), out_shape=...  34.1 us
    unnamed x1, local copies, waits for them, and re-layouts  1.27 us

profile of v7, /device:TPU:1, one launch (start us, length us, event | category | flops | bytes accessed | tf_op | source)
XLA Modules:
  0.0 35.4 jit_solution(15276095695281599864)
XLA Ops:
  0.0 34.1 %shard_map.73 = f32[60,60,128]{2,1,0:T(8,128)S(1)} custom-call(f32[60,64,128]{2,1,0:T(8,128)} %bitcast.8, f32[64,128]{1,0:T(8,128)} %weights_hbm.1, s32[1,128]{1,0:T(1,128)} %bitcast.9, f32[1,128]{1,0:T(1,128)} %bitcast.10, f32[1,128]{1,0:T(1,128)} %bitcast.11, s32[1,128]{1,0:T(1,128)} %bitcast.12, s32[1,128]{1,0:T(1,128)} %bitcast.13), custom_call_target="tpu_custom_call" | custom-call | tf_op jit(solution)/shard_map/pallas_call | solution.py:255
  34.1 1.3 %copy.9 = f32[60,60,128]{2,1,0:T(8,128)} copy(f32[60,60,128]{2,1,0:T(8,128)S(1)} %shard_map.73) | data formatting | bytes 3686400

commit v8 on v7

--- a/solution.py
+++ b/solution.py
@@ -13,7 +13,7 @@
 NQB = 8
 LANES = 128
 CAP = 2
-ROWS = (4, 6, 6, 6, 7)
+ROWS = (4, 6, 6, 8, 5)
 STARTS = tuple(LANES * (sum(ROWS[:c]) // CAP) for c in range(len(ROWS)))
 PITCH = 20
 MESH = pl.DeviceIdType.MESH

time: 35.6 us -> 35.6 us (level)
  no operation moved by 1% of the time
where the time goes in v8:
time: 35.6 us; the launch traced here: 35.5 us
  Pallas kernels  34.2 us (96%)
  local copies, waits for them, and re-layouts  1.27 us (4%)
    pallas_call x1, Pallas kernels, shards(): pl.pallas_call(functools.partial(exchange_kernel, nrow, ncol), out_shape=...  34.2 us
    unnamed x1, local copies, waits for them, and re-layouts  1.27 us

profile of v8, /device:TPU:1, one launch (start us, length us, event | category | flops | bytes accessed | tf_op | source)
XLA Modules:
  0.0 35.5 jit_solution(15261456114915356613)
XLA Ops:
  0.0 34.2 %shard_map.73 = f32[60,60,128]{2,1,0:T(8,128)S(1)} custom-call(f32[60,64,128]{2,1,0:T(8,128)} %bitcast.8, f32[64,128]{1,0:T(8,128)} %weights_hbm.1, s32[1,128]{1,0:T(1,128)} %bitcast.9, f32[1,128]{1,0:T(1,128)} %bitcast.10, f32[1,128]{1,0:T(1,128)} %bitcast.11, s32[1,128]{1,0:T(1,128)} %bitcast.12, s32[1,128]{1,0:T(1,128)} %bitcast.13), custom_call_target="tpu_custom_call" | custom-call | tf_op jit(solution)/shard_map/pallas_call | solution.py:255
  34.2 1.3 %copy.9 = f32[60,60,128]{2,1,0:T(8,128)} copy(f32[60,60,128]{2,1,0:T(8,128)S(1)} %shard_map.73) | data formatting | bytes 3686400
